TPU v7x, 512 devices: a whole 4x4x16 slice. The times are simulated.
512 devices in a mesh: ref: 16 (over x, y_lo, core), dom: 32 (over z, y_hi).
Axes of the slice: x: 4, y: 4 (y_hi: 2, y_lo: 2; y = y_hi * 2 + y_lo), z: 16, core: 2. Of those that a mesh axis runs over, the one named last changes fastest.
Arguments:
- particles: bfloat16 [8192, 7168], P(('ref', 'dom')), may hold values from -16 to 16
- offsets: int32 [8192], P(('ref', 'dom')), may hold values from 0 to 8, as said below
- references: bfloat16 [512, 7168], P('ref'), may hold values from -0.6 to 0.6
- noise_weight: float32 [3584], replicated, may hold values from 0.06 to 0.24
- ref_class: int32 [512], replicated, may hold values from 0 to 7
- ref_orient: int32 [512], replicated, may hold values from 0 to 63
- class_logprior: float32 [8], replicated, may hold values from -1 to 1
- orient_logprior: float32 [64], replicated, may hold values from -1 to 1
Outputs:
- log_post: float32 [8192, 9, 512], P(('ref', 'dom'))
- class_sums: float32 [8, 7168], P(None, ('ref', 'dom'))
Inputs may be any that keep to these rules, and one draw needn't show every extreme that they name: `offsets`: index of the prior's centre: horizontal step (o mod 3) - 1 pixels, vertical step floor(o / 3) - 1 pixels.
All inputs are finite; a program needn't handle non-finite values.
Results may differ from a plain program's by a relative error of at most 0.0042.
Values may be sent and summed in bfloat16 or wider, within the bound.
A program may use at most 64 MiB of HBM per device.

v0:
```python
import math

import jax
import jax.numpy as jnp
from jax import lax
from jax.sharding import PartitionSpec as P

SHIFTS = 9


def in_blocks(shard, dim, length):
    before, after = (shard.shape[:dim], shard.shape[dim + 1 :])
    return jnp.moveaxis(shard.reshape(*before, length, -1, *after), dim, 0)


def sum_at_owner(shard, axis, dim):
    length = lax.axis_size(axis)
    blocks = lax.all_to_all(in_blocks(shard, dim, length), axis, 0, 0, tiled=True)
    return jnp.sum(blocks, axis=0)


def shift_tables(count):
    coeffs = jnp.arange(count, dtype=jnp.int32)
    column_freq = (coeffs % 56).astype(jnp.float32)
    row_freq = (coeffs // 56 - 32).astype(jnp.float32)
    shift_ids = jnp.arange(SHIFTS, dtype=jnp.int32)
    step_right = (shift_ids % 3 - 1).astype(jnp.float32)
    step_down = (shift_ids // 3 - 1).astype(jnp.float32)
    turning = (
        2.0
        * math.pi
        / 96.0
        * (step_right[:, None] * column_freq[None, :] + step_down[:, None] * row_freq[None, :])
    )
    return (jnp.cos(turning), jnp.sin(turning))


def centre_prior(offsets):
    shift_ids = jnp.arange(SHIFTS, dtype=jnp.int32)
    step_right = (shift_ids % 3 - 1).astype(jnp.float32)
    step_down = (shift_ids // 3 - 1).astype(jnp.float32)
    centre_right = (offsets % 3 - 1).astype(jnp.float32)
    centre_down = (offsets // 3 - 1).astype(jnp.float32)
    apart_right = step_right[None, :] - centre_right[:, None]
    apart_down = step_down[None, :] - centre_down[:, None]
    return -0.5 * (apart_right * apart_right + apart_down * apart_down)


def aligned_stack(real_part, imag_part, cosine_table, sine_table, twice):
    turned_real = (
        real_part[:, None, :] * cosine_table[None] - imag_part[:, None, :] * sine_table[None]
    )
    turned_imag = (
        real_part[:, None, :] * sine_table[None] + imag_part[:, None, :] * cosine_table[None]
    )
    stacked_rows = real_part.shape[0] * cosine_table.shape[0]
    scaled_real = (
        (turned_real * twice[None, None, :])
        .astype(jnp.bfloat16)
        .reshape(stacked_rows, real_part.shape[1])
    )
    scaled_imag = (
        (turned_imag * twice[None, None, :])
        .astype(jnp.bfloat16)
        .reshape(stacked_rows, real_part.shape[1])
    )
    return (scaled_real, scaled_imag)


def contract(left, right):
    return lax.dot_general(
        left, right, (((1,), (1,)), ((), ())), preferred_element_type=jnp.float32
    )


def local(
    particles,
    offsets,
    references,
    noise_weight,
    ref_class,
    ref_orient,
    class_logprior,
    orient_logprior,
):
    local_rows = particles.shape[0]
    coef_total = particles.shape[1] // 2
    ref_total = ref_class.shape[0]
    class_count = class_logprior.shape[0]
    cosine_table, sine_table = shift_tables(coef_total)
    twice = 2.0 * noise_weight
    values = particles.astype(jnp.float32)
    real_part = values[:, :coef_total]
    imag_part = values[:, coef_total:]
    scaled_real, scaled_imag = aligned_stack(real_part, imag_part, cosine_table, sine_table, twice)
    class_table = (ref_class[:, None] == jnp.arange(class_count, dtype=jnp.int32)[None, :]).astype(
        jnp.float32
    )
    orient_table = (
        ref_orient[:, None] == jnp.arange(orient_logprior.shape[0], dtype=jnp.int32)[None, :]
    ).astype(jnp.float32)
    prior = jnp.dot(class_table, class_logprior, precision=lax.Precision.HIGHEST) + jnp.dot(
        orient_table, orient_logprior, precision=lax.Precision.HIGHEST
    )
    segment = lax.all_gather(references, "ref", axis=0, tiled=True)
    cross_piece = contract(scaled_real, segment[:, :coef_total]) + contract(
        scaled_imag, segment[:, coef_total:]
    )
    wide = segment.astype(jnp.float32)
    norm_piece = jnp.sum(
        noise_weight[None, :]
        * (
            wide[:, :coef_total] * wide[:, :coef_total]
            + wide[:, coef_total:] * wide[:, coef_total:]
        ),
        axis=1,
    )
    scores = (
        cross_piece.reshape(local_rows, SHIFTS, ref_total)
        - norm_piece[None, None, :]
        + prior[None, None, :]
        + centre_prior(offsets)[:, :, None]
    )
    row_peak = jnp.max(scores, axis=(1, 2), keepdims=True)
    log_total = row_peak + jnp.log(jnp.sum(jnp.exp(scores - row_peak), axis=(1, 2), keepdims=True))
    log_post = scores - log_total
    class_post = jnp.dot(
        jnp.exp(log_post).reshape(local_rows * SHIFTS, ref_total),
        class_table,
        precision=lax.Precision.HIGHEST,
    ).reshape(local_rows, SHIFTS, class_count)
    sums_real = jnp.einsum("ntc,nk->tck", class_post, real_part, precision=lax.Precision.HIGHEST)
    sums_imag = jnp.einsum("ntc,nk->tck", class_post, imag_part, precision=lax.Precision.HIGHEST)
    class_real = jnp.einsum(
        "tk,tck->ck", cosine_table, sums_real, precision=lax.Precision.HIGHEST
    ) - jnp.einsum("tk,tck->ck", sine_table, sums_imag, precision=lax.Precision.HIGHEST)
    class_imag = jnp.einsum(
        "tk,tck->ck", sine_table, sums_real, precision=lax.Precision.HIGHEST
    ) + jnp.einsum("tk,tck->ck", cosine_table, sums_imag, precision=lax.Precision.HIGHEST)
    devices = lax.axis_size(("ref", "dom"))
    partial_value = jnp.concatenate([class_real, class_imag], axis=1) * (
        1.0 / math.sqrt(local_rows * devices)
    )
    by_ref = sum_at_owner(partial_value, "ref", 1)
    class_sums = sum_at_owner(by_ref, "dom", 1)
    return (log_post, class_sums)


def solution(mesh):
    return jax.shard_map(
        local,
        mesh=mesh,
        in_specs=(
            P(("ref", "dom"), None),
            P(("ref", "dom")),
            P("ref", None),
            P(),
            P(),
            P(),
            P(),
            P(),
        ),
        out_specs=(P(("ref", "dom"), None, None), P(None, ("ref", "dom"))),
        check_vma=False,
    )
```

profile of v0, /device:TPU:1, one launch (start us, length us, event | category | flops | bytes accessed | tf_op | source)
XLA Modules:
  0.0 146.9 jit_solution(8516085216977881511)
XLA Ops:
  7.2 0.7 all-gather.2.cloned.1.call-update
  8.0 0.7 fusion.43
  9.2 1.0 fusion.46
  10.1 1.6 %fusion.23 = (f32[3584,9]{0,1:T(8,128)S(1)}, f32[3584,9]{0,1:T(8,128)}, f32[9,3584]{1,0:T(8,128)S(1)}, f32[9,3584]{1,0:T(8,128)S(1)}) fusion(f32[3584]{0:T(1024)S(1)} %get-tuple-element.26, f32[9]{0:T(128)S(1)} %get-tuple-element.29, f32[3584]{0:T(1024)S(1)} %get-tuple-element.27, f32[9]{0:T(128)S(1)} %get-tuple-element.28), kind=kLoop, calls=%fused_computation.43 | loop fusion | flops 129024 | bytes 544840
  11.7 4.0 %multiply_subtract_fusion = (f32[16,9,3584]{2,1,0:T(8,128)}, f32[16,9,3584]{2,1,0:T(8,128)}) fusion(f32[9,3584]{1,0:T(8,128)S(1)} %get-tuple-element.20, f32[16,3584]{1,0:T(8,128)S(1)} %get-tuple-element.17, f32[9,3584]{1,0:T(8,128)S(1)} %get-tuple-element.21, f32[16,3584]{1,0:T(8,128)S(1)} %get-tuple-element.16), kind=kLoop, calls=%fused_computation.12 | loop fusion | flops 3096576 | bytes 4845568 | tf_op jit(solution)/shard_map/sub | solution.py:51
  15.7 3.2 %add.202 = f32[144,3584]{1,0:T(8,128)} reshape(f32[16,9,3584]{2,1,0:T(8,128)} %get-tuple-element.15) | data formatting | bytes 4128768 | tf_op jit(solution)/shard_map/add | solution.py:54
  19.0 2.3 %sub.231 = f32[144,3584]{1,0:T(8,128)S(1)} reshape(f32[16,9,3584]{2,1,0:T(8,128)} %get-tuple-element.14) | data formatting | bytes 4128768 | tf_op jit(solution)/shard_map/sub | solution.py:51
  21.8 48.8 %all-gather.2.cloned.1.call-done = bf16[512,7168]{1,0:T(8,128)(2,1)} async-done(((bf16[32,7168]{1,0:T(8,128)(2,1)}), bf16[512,7168]{1,0:T(8,128)(2,1)}) %all-gather.2.cloned.1.call-update) | async-done | bytes 7340048 | tf_op jit(solution)/shard_map/all_gather | solution.py:105
  70.6 10.2 %convert_element_type.131 = f32[512,7168]{1,0:T(8,128)} convert(bf16[512,7168]{1,0:T(8,128)(2,1)} %all-gather.2.cloned.1.call-done) | non-fusion elementwise | flops 3670016 | bytes 22020096 | tf_op jit(solution)/shard_map/convert_element_type | solution.py:109
  80.8 6.1 %fusion.2 = f32[512]{0:T(512)S(1)} fusion(f32[512,7168]{1,0:T(8,128)} %convert_element_type.131, f32[3584]{0:T(1024)S(1)} %copy-done.5), kind=kLoop, calls=%fused_computation.3 | loop fusion | flops 9174528 | bytes 14696448 | tf_op jit(solution)/shard_map/reduce_sum | solution.py:110
  86.9 1.2 copy-done.1
  88.2 0.6 copy-done.3
  88.7 1.3 fusion.3
  90.1 1.5 %fusion.16 = (f32[144]{0:T(256)S(1)}, f32[144,512]{1,0:T(8,128)S(1)}) fusion(f32[144]{0:T(256)S(1)} %add_multiply_fusion.2, f32[512]{0:T(512)S(1)} %add.205, f32[512]{0:T(512)S(1)} %fusion.2, f32[144,512]{1,0:T(8,128)S(1)} %fusion.3, bf16[512,7168]{1,0:T(8,128)(2,1)S(1)} %copy-done.1, f32[144,3584]{1,0:T(8,128)S(1)} %sub.231, ...), kind=kOutput, calls=%fused_computation.34 | convolution fusion | flops 529883008 | bytes 6346304 | tf_op jit(solution)/shard_map/dot_general | solution.py:71
  92.8 1.0 fusion.34
  94.5 0.7 multiply_reduce_fusion.3
  95.5 0.9 fusion.12
  96.4 5.2 %all-to-all-start = ((f32[16,8,448]{2,1,0:T(8,128)}), f32[16,8,448]{2,1,0:T(8,128)S(1)}, u32[]{:S(2)}, u32[]{:S(2)}) async-start(f32[16,8,448]{2,1,0:T(8,128)} %fusion.12), calls=%async_computation | async-start | bytes 524288 | tf_op jit(solution)/shard_map/all_to_all | solution.py:18
  101.7 7.2 %all-to-all-done = f32[16,8,448]{2,1,0:T(8,128)S(1)} async-done(((f32[16,8,448]{2,1,0:T(8,128)}), f32[16,8,448]{2,1,0:T(8,128)S(1)}, u32[]{:S(2)}, u32[]{:S(2)}) %all-to-all-start) | async-done | bytes 229408 | tf_op jit(solution)/shard_map/all_to_all | solution.py:18
  109.1 0.7 copy.22
  109.8 14.5 %all-to-all-start.1 = ((f32[32,8,14]{2,1,0:T(8,128)}), f32[32,8,14]{2,1,0:T(8,128)S(1)}, u32[]{:S(2)}, u32[]{:S(2)}) async-start(f32[32,8,14]{2,1,0:T(8,128)} %copy.22), calls=%async_computation.1 | async-start | bytes 262144 | tf_op jit(solution)/shard_map/all_to_all | solution.py:18
  124.4 0.9 copy.23
  125.3 14.1 %all-to-all-done.1 = f32[32,8,14]{2,1,0:T(8,128)S(1)} async-done(((f32[32,8,14]{2,1,0:T(8,128)}), f32[32,8,14]{2,1,0:T(8,128)S(1)}, u32[]{:S(2)}, u32[]{:S(2)}) %all-to-all-start.1) | async-done | bytes 14368 | tf_op jit(solution)/shard_map/all_to_all | solution.py:18
  139.5 0.6 reduce_sum.48
  (56 shorter events, 3.6 us)
Async XLA Ops:
  7.2 14.1 %copy-start = (f32[8]{0:T(128)S(1)}, f32[8]{0:T(128)}, u32[]{:S(2)}) copy-start(f32[8]{0:T(128)} %param.14) | copy-start | bytes 100
  7.2 63.4 %all-gather.2.cloned.1.call-start = ((), (), s32[]{:S(2)}) async-start(), calls=%async_computation.2 | async-start | bytes 7798784 | tf_op jit(solution)/shard_map/all_gather | solution.py:105
  19.0 2.3 %copy-start.6 = (s32[512]{0:T(512)S(1)}, s32[512]{0:T(512)}, u32[]{:S(2)}) copy-start(s32[512]{0:T(512)} %param.12) | copy-start | bytes 6148
  19.0 2.5 %copy-start.7 = (s32[512]{0:T(512)S(1)}, s32[512]{0:T(512)}, u32[]{:S(2)}) copy-start(s32[512]{0:T(512)} %param.13) | copy-start | bytes 6148
  19.0 2.5 %copy-start.8 = (f32[64]{0:T(128)S(1)}, f32[64]{0:T(128)}, u32[]{:S(2)}) copy-start(f32[64]{0:T(128)} %param.15) | copy-start | bytes 772
  19.0 2.8 %copy-start.5 = (f32[3584]{0:T(1024)S(1)}, f32[3584]{0:T(1024)}, u32[]{:S(2)}) copy-start(f32[3584]{0:T(1024)} %param.11) | copy-start | bytes 43012
  80.8 7.3 %copy-start.1 = (bf16[512,7168]{1,0:T(8,128)(2,1)S(1)}, bf16[512,7168]{1,0:T(8,128)(2,1)}, u32[]{:S(2)}) copy-start(bf16[512,7168]{1,0:T(8,128)(2,1)} %all-gather.2.cloned.1.call-done) | copy-start | bytes 22020100
  80.8 7.9 %copy-start.3 = (f32[144,3584]{1,0:T(8,128)S(1)}, f32[144,3584]{1,0:T(8,128)}, u32[]{:S(2)}) copy-start(f32[144,3584]{1,0:T(8,128)} %add.202) | copy-start | bytes 6193156
  90.1 3.9 %copy-start.2 = (bf16[16,7168]{1,0:T(8,128)(2,1)S(1)}, bf16[16,7168]{1,0:T(8,128)(2,1)}, u32[]{:S(2)}) copy-start(bf16[16,7168]{1,0:T(8,128)(2,1)} %param.8) | copy-start | bytes 688132
  91.6 2.9 %copy-start.4 = (f32[3584,9]{0,1:T(8,128)S(1)}, f32[3584,9]{0,1:T(8,128)}, u32[]{:S(2)}) copy-start(f32[3584,9]{0,1:T(8,128)} %get-tuple-element.19) | copy-start | bytes 387076
  96.4 12.5 %all-to-all-start = ((f32[16,8,448]{2,1,0:T(8,128)}), f32[16,8,448]{2,1,0:T(8,128)S(1)}, u32[]{:S(2)}, u32[]{:S(2)}) async-start(f32[16,8,448]{2,1,0:T(8,128)} %fusion.12), calls=%async_computation | async-start | bytes 524288 | tf_op jit(solution)/shard_map/all_to_all | solution.py:18
  109.8 29.6 %all-to-all-start.1 = ((f32[32,8,14]{2,1,0:T(8,128)}), f32[32,8,14]{2,1,0:T(8,128)S(1)}, u32[]{:S(2)}, u32[]{:S(2)}) async-start(f32[32,8,14]{2,1,0:T(8,128)} %copy.22), calls=%async_computation.1 | async-start | bytes 262144 | tf_op jit(solution)/shard_map/all_to_all | solution.py:18
Sparse Core Ops, SparseCore 0:
  10.1 60.4 all-gather.1
where the time goes:
time: 148 us; the launch traced here: 147 us
  waiting for transfers between devices  70.9 us (48%)
  other arithmetic  25 us (17%)
  starting transfers between devices  19.6 us (13%)
  between operations  14.3 us (10%)
  local copies, waits for them, and re-layouts  11.5 us (8%)
  matrix products  5.57 us (4%)
    all_gather x1, waiting for transfers between devices, local(): segment = lax.all_gather(references, 'ref', axis=0, tiled=True)  48.8 us
    all_to_all x2, waiting for transfers between devices, sum_at_owner(): lax.all_to_all(in_blocks(shard, dim, length), axis, 0, 0, tiled=True)  21.4 us
    all_to_all x2, starting transfers between devices, sum_at_owner(): lax.all_to_all(in_blocks(shard, dim, length), axis, 0, 0, tiled=True)  19.6 us
    convert_element_type x1, other arithmetic, local(): wide = segment.astype(jnp.float32)  10.2 us
    reduce_sum x1, other arithmetic, local(): jnp.sum(noise_weight[None, :] * (wide[:, :coef_total] * wide[:, :coef_tot...  6.08 us
    sub x1, other arithmetic, aligned_stack(): real_part[:, None, :] * cosine_table[None]  4 us
    add x1, local copies, waits for them, and re-layouts, aligned_stack(): real_part[:, None, :] * sine_table[None]  3.22 us
  transfers between devices with their start and end apart: 3, of which 3 were waited for; matrix products, arithmetic and copies ran while one was open for 10% of the time, Pallas kernels for 0%

commit v1 on v0

v1 whole, which is shorter than its diff:
```python
import functools
import math

import jax
import jax.numpy as jnp
import numpy as np
from jax import lax
from jax.experimental import pallas as pl
from jax.experimental.pallas import tpu as pltpu
from jax.sharding import PartitionSpec as P

MESH = pl.DeviceIdType.MESH
SHIFTS = 9
NX = 4
NS = 4
NZ = 16
NG = 8
NQ = 4
LANES = 128
F32 = jnp.float32
BF16 = jnp.bfloat16
PAIRS = ((5, 3), (7, 1), (8, 0), (6, 2))
STEPS = ((1, 0), (0, 1), (1, 1), (-1, 1))


def phase_tables(count):
    coeffs = np.arange(count)
    fx = (coeffs % 56).astype(np.float32)
    fy = (coeffs // 56 - 32).astype(np.float32)
    rows = []
    for sx, sy in STEPS:
        turning = np.float32(2.0 * math.pi / 96.0) * (np.float32(sx) * fx + np.float32(sy) * fy)
        turning = turning.astype(np.float64)
        rows += [np.cos(turning), np.sin(turning)]
    table = np.stack(rows).astype(np.float32)
    return np.ascontiguousarray(table.reshape(len(rows), -1, LANES).swapaxes(0, 1))


def nt(a, b):
    return lax.dot_general(a, b, (((1,), (1,)), ((), ())), preferred_element_type=F32)


def nn(a, b):
    return lax.dot_general(a, b, (((1,), (0,)), ((), ())), preferred_element_type=F32)


def split(value):
    high = value.astype(BF16)
    return high, (value - high.astype(F32)).astype(BF16)


def kernel(
    coefs,
    npart,
    rows,
    nref,
    classes,
    orients,
    off_hbm,
    clp_hbm,
    olp_hbm,
    part_hbm,
    refs_hbm,
    w_hbm,
    cls_hbm,
    ori_hbm,
    tab_hbm,
    post_out,
    sums_out,
    off,
    clp,
    olp,
    w,
    cls,
    ori,
    tab,
    tw,
    pb,
    rb,
    sp,
    s,
    na,
    spv,
    espb,
    gb,
    lz,
    sr,
    cb,
    wb,
    yb,
    tb,
    zb,
    far,
    sm,
    lp,
    lr,
    s_right,
    s_left,
    s_fwd,
    r_left,
    r_right,
    r_opp,
    s_y,
    s_p,
    s_py,
    r_y,
    r_p,
    r_py,
    s_e,
    r_e,
    s_g,
    r_g,
    s_s,
    r_s,
    s_w,
    r_w,
    s_z,
    r_z,
):
    ck = coefs // NQ
    me = lax.axis_index("ref")
    dm = lax.axis_index("dom")
    x = me // NS
    sub = me % NS
    yl = sub // 2
    core = sub % 2
    z = dm // 2
    yh = dm % 2
    group = sub * 2 + yh
    right = (me + NS) % (NX * NS)
    left = (me + (NX - 1) * NS) % (NX * NS)
    opposite = (me + 2 * NS) % (NX * NS)
    xl = (x + NX - 1) % NX
    xr = (x + 1) % NX
    partner = me + 1 - 2 * core
    y_ref = me + 2 - 4 * yl
    y_dom = dm + core * (1 - 2 * yh)
    refs = nref

    def remote(src, dst, send, recv, ref, dom):
        return pltpu.make_async_remote_copy(
            src_ref=src,
            dst_ref=dst,
            send_sem=send,
            recv_sem=recv,
            device_id=(ref, dom),
            device_id_type=MESH,
        )

    def arrived(buffer, sem):
        pltpu.make_async_copy(buffer, buffer, sem).wait()

    smalls = (
        (off_hbm, off),
        (clp_hbm, clp),
        (olp_hbm, olp),
        (w_hbm, w),
        (cls_hbm, cls),
        (ori_hbm, ori),
        (tab_hbm, tab),
    )
    own_rows = pl.ds(pl.multiple_of(sub * refs, refs), refs)
    for q in range(NQ):
        for half in range(2):
            pltpu.make_async_copy(
                part_hbm.at[:, pl.ds(half * coefs + q * ck, ck)],
                pb.at[x, q, :, pl.ds(half * ck, ck)],
                lp.at[q],
            ).start()
            pltpu.make_async_copy(
                refs_hbm.at[:, pl.ds(half * coefs + q * ck, ck)],
                rb.at[q, own_rows, pl.ds(half * ck, ck)],
                lr.at[q],
            ).start()
    for i, (src, dst) in enumerate(smalls):
        pltpu.make_async_copy(src, dst, sm.at[i]).start()

    barrier = pltpu.get_barrier_semaphore()

    def beside(distance, act):
        @pl.when(z >= distance)
        def _():
            act(me, dm - 2 * distance)

        @pl.when(z + distance < NZ)
        def _():
            act(me, dm + 2 * distance)

    def near(distance):
        return (z + NZ - distance) // NZ + (2 * NZ - 1 - z - distance) // NZ

    def greet(ref, dom):
        pl.semaphore_signal(barrier, inc=1, device_id=(ref, dom), device_id_type=MESH)

    for step in range(1, NX):
        greet((me + step * NS) % (NX * NS), dm)
    for step in range(1, NG):
        other = (group + step) % NG
        greet(x * NS + other // 2, z * 2 + other % 2)
    beside(1, greet)
    pl.semaphore_wait(barrier, NX - 1 + NG - 1 + near(1))

    def tell(i):
        def one(ref, dom):
            pl.semaphore_signal(far.at[i], inc=1, device_id=(ref, dom), device_id_type=MESH)

        beside(2**i, one)

    def heard(i):
        pl.semaphore_wait(far.at[i], near(2**i))

    tell(0)

    sends = []

    def go(copy):
        copy.start()
        sends.append(copy)

    def send_own(q):
        go(remote(pb.at[x, q], pb.at[x, q], s_right.at[q], r_left.at[q], right, dm))
        go(remote(pb.at[x, q], pb.at[x, q], s_left.at[q], r_right.at[q], left, dm))

    def forward(q):
        if q % 2 == 0:
            arrived(pb.at[xl, q], r_left.at[q])
            go(remote(pb.at[xl, q], pb.at[xl, q], s_fwd.at[q], r_opp.at[q], right, dm))
        else:
            arrived(pb.at[xr, q], r_right.at[q])
            go(remote(pb.at[xr, q], pb.at[xr, q], s_fwd.at[q], r_opp.at[q], left, dm))

    y_rows = pl.ds(pl.multiple_of((y_ref % NS) * refs, refs), refs)
    p_rows = pl.ds(pl.multiple_of((partner % NS) * refs, refs), refs)
    py_sub = (partner % NS) + 2 - 4 * yl
    py_rows = pl.ds(pl.multiple_of(py_sub * refs, refs), refs)

    for q in range(NQ):
        arrived(pb.at[x, q], lp.at[q])
        arrived(rb.at[q, own_rows], lr.at[q])
        if q < 2:
            send_own(q)
        own = rb.at[q, own_rows]
        go(remote(own, own, s_y.at[q], r_y.at[q], y_ref, y_dom))
        go(remote(own, own, s_p.at[q], r_p.at[q], partner, dm))

    for i, (src, dst) in enumerate(smalls):
        pltpu.make_async_copy(src, dst, sm.at[i]).wait()
    for i in range(coefs // LANES):
        two_w = 2.0 * w[i : i + 1, :]
        tw[i, 0:8, :] = tab[i] * two_w
        tw[i, 8:9, :] = two_w
    lane = lax.broadcasted_iota(jnp.int32, (1, LANES), 1)
    shift = lane // classes
    step_right = (shift % 3 - 1).astype(F32)
    step_down = (shift // 3 - 1).astype(F32)
    for n in range(rows):
        o = off[n]
        down = jnp.where(o >= 6, 2, jnp.where(o >= 3, 1, 0))
        centre_right = (o - 3 * down - 1).astype(F32)
        centre_down = (down - 1).astype(F32)
        apart_right = step_right - centre_right
        apart_down = step_down - centre_down
        spv[n : n + 1, :] = -0.5 * (apart_right * apart_right + apart_down * apart_down)
    used = lane < SHIFTS * classes
    espb[x] = jnp.where(used, jnp.exp(spv[...]), 0.0)
    for step, peer in enumerate((right, left, opposite)):
        go(remote(espb.at[x], espb.at[x], s_e.at[step], r_e.at[step], peer, dm))
    class_row = cls[pl.ds(x, 1), :]
    orient_row = ori[pl.ds(x, 1), :]
    prior = jnp.zeros((1, LANES), F32)
    for i in range(classes):
        prior = prior + jnp.where(class_row == i, clp[i], 0.0)
    orient_prior = jnp.zeros((1, LANES), F32)
    for i in range(orients):
        orient_prior = orient_prior + jnp.where(orient_row == i, olp[i], 0.0)
    prior = prior + orient_prior
    na[...] = jnp.zeros_like(na)
    s[...] = jnp.zeros_like(s)

    def compute(q):
        def tile(j, carry):
            at_real = pl.ds(pl.multiple_of(j * LANES, LANES), LANES)
            at_imag = pl.ds(pl.multiple_of(ck + j * LANES, LANES), LANES)
            at_table = q * (ck // LANES) + j
            real = pb[:, q, :, at_real].reshape(NX * rows, LANES).astype(F32)
            imag = pb[:, q, :, at_imag].reshape(NX * rows, LANES).astype(F32)

            def put(t, turned_real, turned_imag):
                sp[pl.ds(t * NX * rows, NX * rows), at_real] = turned_real.astype(BF16)
                sp[pl.ds(t * NX * rows, NX * rows), at_imag] = turned_imag.astype(BF16)

            plain = tw[at_table, 8:9, :]
            put(4, real * plain, imag * plain)
            for i, (plus, minus) in enumerate(PAIRS):
                cosine = tw[at_table, 2 * i : 2 * i + 1, :]
                sine = tw[at_table, 2 * i + 1 : 2 * i + 2, :]
                rc, rs = real * cosine, real * sine
                ic, is_ = imag * cosine, imag * sine
                put(plus, rc - is_, rs + ic)
                put(minus, rc + is_, ic - rs)
            weight = w[pl.ds(at_table, 1), :]
            ref_real = rb[q, :, at_real].astype(F32)
            ref_imag = rb[q, :, at_imag].astype(F32)
            na[...] += weight * (ref_real * ref_real + ref_imag * ref_imag)
            return carry

        lax.fori_loop(0, ck // LANES, tile, 0)
        s[...] += nt(sp[...], rb[q])

    def forward_refs(q):
        arrived(rb.at[q, y_rows], r_y.at[q])
        there = rb.at[q, y_rows]
        go(remote(there, there, s_py.at[q], r_py.at[q], partner, dm))

    def ready(q):
        if q % 2 == 0:
            arrived(pb.at[xr, q], r_right.at[q])
        else:
            arrived(pb.at[xl, q], r_left.at[q])
        arrived(pb.at[xl, q], r_opp.at[q])
        arrived(rb.at[q, p_rows], r_p.at[q])
        arrived(rb.at[q, py_rows], r_py.at[q])

    forward(0)
    send_own(2)
    forward_refs(0)
    forward(1)
    send_own(3)
    heard(0)
    tell(1)
    forward_refs(1)
    ready(0)
    compute(0)
    heard(1)
    tell(2)
    forward(2)
    forward_refs(2)
    ready(1)
    compute(1)
    forward(3)
    forward_refs(3)
    ready(2)
    compute(2)
    heard(2)
    tell(3)
    ready(3)
    compute(3)

    norm_row = jnp.sum(na[...].T, axis=0, keepdims=True)
    s[...] += prior - norm_row
    parts = NX * rows
    peak = s[0:parts, :]
    for t in range(1, SHIFTS):
        peak = jnp.maximum(peak, s[t * parts : (t + 1) * parts, :])
    peak = jnp.max(peak, axis=1, keepdims=True)
    column = lax.broadcasted_iota(jnp.int32, (LANES, LANES), 0)
    member = column % classes == class_row
    sums = jnp.zeros((parts, LANES), F32)
    for t in range(SHIFTS):
        chosen = jnp.where(member & (column // classes == t), 1.0, 0.0).astype(BF16)
        high, low = split(jnp.exp(s[t * parts : (t + 1) * parts, :] - peak))
        sums = sums + (nt(high, chosen) + nt(low, chosen))
    gb[x] = jnp.where(used, sums, peak)
    for step, peer in enumerate((right, left, opposite)):
        go(remote(gb.at[x], gb.at[x], s_g.at[step], r_g.at[step], peer, dm))
    s4 = s.reshape(SHIFTS, NX, rows, LANES)
    for step, peer in enumerate((right, left, opposite)):
        go(
            remote(
                s4.at[:, (x + (1, NX - 1, 2)[step]) % NX],
                sr.at[x],
                s_s.at[step],
                r_s.at[step],
                peer,
                dm,
            )
        )
    sr[x] = s4[:, x]

    for step in range(3):
        src = (x + (NX - 1, 1, 2)[step]) % NX
        arrived(espb.at[src], r_e.at[step])
    for step in range(3):
        src = (x + (NX - 1, 1, 2)[step]) % NX
        arrived(gb.at[src], r_g.at[step])
    peaks = [gb[i][:, LANES - 1 : LANES] for i in range(NX)]
    top = jnp.maximum(jnp.maximum(peaks[0], peaks[1]), jnp.maximum(peaks[2], peaks[3]))
    total = jnp.zeros((parts, LANES), F32)
    for i in range(NX):
        total = total + gb[i] * jnp.exp(peaks[i] - top)
    total = jnp.where(used, total, 0.0) * espb[...].reshape(parts, LANES)
    norm = jnp.sum(total, axis=1, keepdims=True)
    post = total * (1.0 / norm)
    lz[...] = jnp.broadcast_to(top + jnp.log(norm), (parts, LANES))

    turned = jnp.concatenate([post, jnp.zeros((LANES - parts, LANES), F32)], axis=0).T
    high, low = split(turned[: SHIFTS * classes, :parts])
    real_side = x < NX // 2
    at_e = pl.ds(pl.multiple_of(jnp.where(real_side, 0, ck), LANES), ck)
    at_f = pl.ds(pl.multiple_of(jnp.where(real_side, ck, 0), LANES), ck)
    sign = jnp.where(real_side, -1.0, 1.0).astype(F32) * (1.0 / math.sqrt(npart))
    scale = 1.0 / math.sqrt(npart)
    for piece in range(NQ // 2):
        q = (x % 2) * (NQ // 2) + piece
        e_rows = pb[:, q, :, at_e].reshape(parts, ck)
        f_rows = pb[:, q, :, at_f].reshape(parts, ck)
        e = nn(high, e_rows) + nn(low, e_rows)
        f = nn(high, f_rows) + nn(low, f_rows)
        for j in range(ck // LANES):
            at_table = q * (ck // LANES) + j

            def of(table, t):
                return table[t * classes : (t + 1) * classes, j * LANES : (j + 1) * LANES]

            even = of(e, 4)
            odd = jnp.zeros((classes, LANES), F32)
            for i, (plus, minus) in enumerate(PAIRS):
                cosine = tab[at_table, 2 * i : 2 * i + 1, :]
                sine = tab[at_table, 2 * i + 1 : 2 * i + 2, :]
                even = even + cosine * (of(e, plus) + of(e, minus))
                odd = odd + sine * (of(f, plus) - of(f, minus))
            at_column = piece * ck + j * LANES
            cb[:, at_column : at_column + LANES] = scale * even + sign * odd

    width = 2 * coefs // NX
    cols = width // LANES
    spread = LANES // classes
    k = lax.broadcasted_iota(jnp.int32, (spread, width), 1)
    keep = k % cols == lax.broadcasted_iota(jnp.int32, (spread, width), 0)
    d = lax.broadcasted_iota(jnp.int32, (LANES, width), 0)
    first = ((d // 32) * 32 + (d % 16) * 2 + (d // 16) % 2) * cols
    k = lax.broadcasted_iota(jnp.int32, (LANES, width), 1)
    pick = jnp.where((k >= first) & (k < first + cols), 1.0, 0.0).astype(BF16)
    laid = jnp.concatenate(
        [
            jnp.where(keep, jnp.broadcast_to(cb[i : i + 1, :], (spread, width)), 0.0)
            for i in [0, *range(classes - 1, 0, -1)]
        ],
        axis=0,
    )
    high, low = split(laid)
    wb[...] = (nt(pick, high) + nt(pick, low)).reshape(NG, NZ, LANES)
    for step in range(1, NG):
        other = (group + step) % NG
        go(
            remote(
                wb.at[other],
                yb.at[group],
                s_w.at[step],
                r_w.at[group],
                x * NS + other // 2,
                z * 2 + other % 2,
            )
        )
    yb[group] = wb[group]
    for step in range(1, NG):
        src = (group + step) % NG
        arrived(yb.at[src], r_w.at[src])
    heard(3)
    tb[...] = jnp.sum(yb[...], axis=0).reshape(NZ, 1, LANES)
    for step in range(1, NZ):
        other = (z + step) % NZ
        go(remote(tb.at[other], zb.at[z], s_z.at[step], r_z.at[z], me, other * 2 + yh))
    zb[z] = tb[z]

    for step in range(3):
        src = (x + (NX - 1, 1, 2)[step]) % NX
        arrived(sr.at[src], r_s.at[step])
    own_z = lz[pl.ds(pl.multiple_of(x * rows, rows), rows), :]
    for t in range(SHIFTS):
        bias = spv[:, t * classes : t * classes + 1] - own_z
        for i in range(NX):
            post_out[t, :, i * LANES : (i + 1) * LANES] = sr[i, t] + bias

    for step in range(1, NZ):
        src = (z + step) % NZ
        arrived(zb.at[src], r_z.at[src])
    final = jnp.sum(zb[...], axis=0)
    final = jnp.broadcast_to(final, (classes, LANES))
    final = pltpu.roll(final, 0, 1, stride=spread, stride_axis=0)
    sums_out[...] = final[:, :cols]
    for copy in sends:
        copy.wait_send()


def solution(mesh):
    assert mesh.shape["ref"] == NX * NS and mesh.shape["dom"] == 2 * NZ

    def local(particles, offsets, references, noise_weight, ref_class, ref_orient, class_logprior, orient_logprior):
        rows, both = particles.shape
        coefs = both // 2
        refs = references.shape[0]
        classes = class_logprior.shape[0]
        orients = orient_logprior.shape[0]
        ck = coefs // NQ
        parts = NX * rows
        width = both // NX
        cols = width // LANES
        npart = rows * NX * NS * 2 * NZ
        assert ck % LANES == 0 and refs * NS == LANES and SHIFTS * classes < LANES
        dma = pltpu.SemaphoreType.DMA
        log_post, class_sums = pl.pallas_call(
            functools.partial(kernel, coefs, npart, rows, refs, classes, orients),
            out_shape=(
                jax.ShapeDtypeStruct((SHIFTS, rows, NX * LANES), F32),
                jax.ShapeDtypeStruct((classes, cols), F32),
            ),
            in_specs=[pl.BlockSpec(memory_space=pltpu.HBM)] * 9,
            out_specs=(
                pl.BlockSpec(memory_space=pltpu.VMEM),
                pl.BlockSpec(memory_space=pltpu.VMEM),
            ),
            scratch_shapes=[
                pltpu.SMEM((rows,), jnp.int32),
                pltpu.SMEM((classes,), F32),
                pltpu.SMEM((orients,), F32),
                pltpu.VMEM((coefs // LANES, LANES), F32),
                pltpu.VMEM((NX, LANES), jnp.int32),
                pltpu.VMEM((NX, LANES), jnp.int32),
                pltpu.VMEM((coefs // LANES, 8, LANES), F32),
                pltpu.VMEM((coefs // LANES, 16, LANES), F32),
                pltpu.VMEM((NX, NQ, rows, 2 * ck), BF16),
                pltpu.VMEM((NQ, LANES, 2 * ck), BF16),
                pltpu.VMEM((SHIFTS * parts, 2 * ck), BF16),
                pltpu.VMEM((SHIFTS * parts, LANES), F32),
                pltpu.VMEM((LANES, LANES), F32),
                pltpu.VMEM((rows, LANES), F32),
                pltpu.VMEM((NX, rows, LANES), F32),
                pltpu.VMEM((NX, parts, LANES), F32),
                pltpu.VMEM((parts, LANES), F32),
                pltpu.VMEM((NX, SHIFTS, rows, LANES), F32),
                pltpu.VMEM((classes, width), F32),
                pltpu.VMEM((NG, NZ, LANES), F32),
                pltpu.VMEM((NG, NZ, LANES), F32),
                pltpu.VMEM((NZ, 1, LANES), F32),
                pltpu.VMEM((NZ, 1, LANES), F32),
                pltpu.SemaphoreType.REGULAR((4,)),
                dma((7,)),
            ]
            + [dma((NQ,))] * 14
            + [dma((3,))] * 6
            + [dma((NG,))] * 2
            + [dma((NZ,))] * 2,
            compiler_params=pltpu.CompilerParams(
                collective_id=0, has_side_effects=True, vmem_limit_bytes=67043328
            ),
            name="expectation",
        )(
            offsets,
            class_logprior,
            orient_logprior,
            particles,
            references,
            noise_weight.reshape(coefs // LANES, LANES),
            ref_class.reshape(NX, LANES),
            ref_orient.reshape(NX, LANES),
            jnp.asarray(phase_tables(coefs)),
        )
        return jnp.swapaxes(log_post, 0, 1), class_sums

    return jax.shard_map(
        local,
        mesh=mesh,
        in_specs=(
            P(("ref", "dom"), None),
            P(("ref", "dom")),
            P("ref", None),
            P(),
            P(),
            P(),
            P(),
            P(),
        ),
        out_specs=(P(("ref", "dom"), None, None), P(None, ("ref", "dom"))),
        check_vma=False,
    )
```

time: 148 us -> 51.9 us (0.35)
  waiting for transfers between devices: 70.9 us -> 0 us
  Pallas kernels: 0 us -> 48.8 us
  other arithmetic: 25 us -> 0 us
  starting transfers between devices: 19.6 us -> 0 us
  between operations: 14.3 us -> 0.65 us
  local copies, waits for them, and re-layouts: 11.5 us -> 2.29 us
  matrix products: 5.57 us -> 0 us
    all_gather x1 -> x0, waiting for transfers between devices: 48.8 us -> none  [local(): segment = lax.all_gather(references, 'ref', axis=0, tiled=True)]
    pallas_call x0 -> x1, Pallas kernels: none -> 48.8 us  [local(): pl.pallas_call(functools.partial(kernel, coefs, npart, rows, refs, classe...]
    all_to_all x2 -> x0, waiting for transfers between devices: 21.4 us -> none  [sum_at_owner(): lax.all_to_all(in_blocks(shard, dim, length), axis, 0, 0, tiled=True)]
    all_to_all x2 -> x0, starting transfers between devices: 19.6 us -> none  [sum_at_owner(): lax.all_to_all(in_blocks(shard, dim, length), axis, 0, 0, tiled=True)]
    convert_element_type x4 -> x0, other arithmetic: 10.9 us -> none  [the longest x1 10.2 us: local(): wide = segment.astype(jnp.float32)]
    reduce_sum x5 -> x0, other arithmetic: 7.08 us -> none  [the longest x1 6.08 us: local(): jnp.sum(noise_weight[None, :] * (wide[:, :coef_total] * wide[:, :coef_tot...]
    dot_general x7 -> x0, matrix products: 5.57 us -> none  [the longest x2 2.82 us: contract(): lax.dot_general(left, right, (((1,), (1,)), ((), ())), preferred_element_...]
    sub x3 -> x0, other arithmetic: 4.16 us -> none  [the longest x1 4 us: aligned_stack(): real_part[:, None, :] * cosine_table[None]]
  transfers between devices with their start and end apart: 3 -> 0, of which waited for: 3 -> 0; matrix products, arithmetic and copies ran while one was open for 10% -> 0% of each run, Pallas kernels for 0% -> 0%
where the time goes in v1:
time: 51.9 us; the launch traced here: 51.7 us
  Pallas kernels  48.8 us (94%)
  local copies, waits for them, and re-layouts  2.29 us (4%)
  between operations  0.65 us (1%)
    pallas_call x1, Pallas kernels, local(): pl.pallas_call(functools.partial(kernel, coefs, npart, rows, refs, classe...  48.8 us
    unnamed x4, local copies, waits for them, and re-layouts  2.29 us

profile of v1, /device:TPU:1, one launch (start us, length us, event | category | flops | bytes accessed | tf_op | source)
XLA Modules:
  0.0 51.7 jit_solution(6100590603892201571)
XLA Ops:
  0.6 48.8 %expectation.1 = (f32[9,16,512]{2,1,0:T(8,128)}, f32[8,14]{1,0:T(8,128)}) custom-call(s32[16]{0:T(128)} %off_hbm.1, f32[8]{0:T(128)} %clp_hbm.1, f32[64]{0:T(128)} %olp_hbm.1, bf16[16,7168]{1,0:T(8,128)(2,1)} %part_hbm.1, bf16[32,7168]{1,0:T(8,128)(2,1)} %refs_hbm.1, f32[28,128]{1,0:T(8,128)} %bitcast.5, s32[4,128]{1,0:T(4,128)} %bitcast.6, ...), custom_call_target="tpu_custom_call" | custom-call | tf_op jit(solution)/shard_map/expectation/pallas_call | solution.py:502
  49.4 0.0 copy-start
  49.4 1.7 %copy.13 = f32[16,9,512]{2,0,1:T(8,128)} copy(f32[16,9,512]{2,0,1:T(8,128)} %bitcast.4) | data formatting | bytes 589824
  51.1 0.0 copy-done
  51.1 0.6 %copy.14 = f32[8,14]{1,0:T(8,128)} copy(f32[8,14]{1,0:T(8,128)S(1)} %copy-done) | data formatting | bytes 896
Async XLA Ops:
  49.4 1.7 %copy-start = (f32[8,14]{1,0:T(8,128)S(1)}, f32[8,14]{1,0:T(8,128)}, u32[]{:S(2)}) copy-start(f32[8,14]{1,0:T(8,128)} %get-tuple-element.9) | copy-start | bytes 1348

commit v2 on v1

--- a/solution.py
+++ b/solution.py
@@ -15,7 +15,8 @@
 NS = 4
 NZ = 16
 NG = 8
-NQ = 4
+NQ = 7
+AHEAD = 5
 LANES = 128
 F32 = jnp.float32
 BF16 = jnp.bfloat16
@@ -84,6 +85,9 @@
     espb,
     gb,
     lz,
+    chosen,
+    keep,
+    pick,
     sr,
     cb,
     wb,
@@ -236,9 +240,9 @@
 
     for q in range(NQ):
         arrived(pb.at[x, q], lp.at[q])
+        if q < AHEAD:
+            send_own(q)
         arrived(rb.at[q, own_rows], lr.at[q])
-        if q < 2:
-            send_own(q)
         own = rb.at[q, own_rows]
         go(remote(own, own, s_y.at[q], r_y.at[q], y_ref, y_dom))
         go(remote(own, own, s_p.at[q], r_p.at[q], partner, dm))
@@ -274,6 +278,19 @@
     for i in range(orients):
         orient_prior = orient_prior + jnp.where(orient_row == i, olp[i], 0.0)
     prior = prior + orient_prior
+    column = lax.broadcasted_iota(jnp.int32, (LANES, LANES), 0)
+    member = column % classes == class_row
+    for t in range(SHIFTS):
+        chosen[:, t * LANES : (t + 1) * LANES] = jnp.where(member & (column // classes == t), 1.0, 0.0).astype(BF16)
+    width = 2 * coefs // NX
+    cols = width // LANES
+    spread = LANES // classes
+    k = lax.broadcasted_iota(jnp.int32, (spread, width), 1)
+    keep[...] = jnp.where(k % cols == lax.broadcasted_iota(jnp.int32, (spread, width), 0), 1.0, 0.0)
+    d = lax.broadcasted_iota(jnp.int32, (LANES, width), 0)
+    first = ((d // 32) * 32 + (d % 16) * 2 + (d // 16) % 2) * cols
+    k = lax.broadcasted_iota(jnp.int32, (LANES, width), 1)
+    pick[...] = jnp.where((k >= first) & (k < first + cols), 1.0, 0.0).astype(BF16)
     na[...] = jnp.zeros_like(na)
     s[...] = jnp.zeros_like(s)
 
@@ -322,29 +339,29 @@
         arrived(rb.at[q, py_rows], r_py.at[q])
 
     forward(0)
-    send_own(2)
+    send_own(AHEAD)
     forward_refs(0)
-    forward(1)
-    send_own(3)
     heard(0)
     tell(1)
+    forward(1)
+    for q in range(AHEAD + 1, NQ):
+        send_own(q)
     forward_refs(1)
-    ready(0)
-    compute(0)
-    heard(1)
-    tell(2)
     forward(2)
-    forward_refs(2)
-    ready(1)
-    compute(1)
     forward(3)
-    forward_refs(3)
-    ready(2)
-    compute(2)
-    heard(2)
-    tell(3)
-    ready(3)
-    compute(3)
+    for q in range(NQ):
+        if q + 2 < NQ:
+            forward_refs(q + 2)
+        ready(q)
+        if q + 4 < NQ:
+            forward(q + 4)
+        compute(q)
+        if q == 1:
+            heard(1)
+            tell(2)
+        if q == 4:
+            heard(2)
+            tell(3)
 
     norm_row = jnp.sum(na[...].T, axis=0, keepdims=True)
     s[...] += prior - norm_row
@@ -353,14 +370,12 @@
     for t in range(1, SHIFTS):
         peak = jnp.maximum(peak, s[t * parts : (t + 1) * parts, :])
     peak = jnp.max(peak, axis=1, keepdims=True)
-    column = lax.broadcasted_iota(jnp.int32, (LANES, LANES), 0)
-    member = column % classes == class_row
-    sums = jnp.zeros((parts, LANES), F32)
-    for t in range(SHIFTS):
-        chosen = jnp.where(member & (column // classes == t), 1.0, 0.0).astype(BF16)
-        high, low = split(jnp.exp(s[t * parts : (t + 1) * parts, :] - peak))
-        sums = sums + (nt(high, chosen) + nt(low, chosen))
-    gb[x] = jnp.where(used, sums, peak)
+    peak_high, peak_low = split(peak)
+    peak = peak_high.astype(F32) + peak_low.astype(F32)
+    powers = [jnp.exp(s[t * parts : (t + 1) * parts, :] - peak).astype(BF16) for t in range(SHIFTS)]
+    sums = nt(jnp.concatenate(powers, axis=1), chosen[...])
+    tail = jnp.where(lane < LANES - 1, peak_high.astype(F32), peak_low.astype(F32))
+    gb[x] = jnp.where(used, sums, tail).astype(BF16)
     for step, peer in enumerate((right, left, opposite)):
         go(remote(gb.at[x], gb.at[x], s_g.at[step], r_g.at[step], peer, dm))
     s4 = s.reshape(SHIFTS, NX, rows, LANES)
@@ -383,31 +398,36 @@
     for step in range(3):
         src = (x + (NX - 1, 1, 2)[step]) % NX
         arrived(gb.at[src], r_g.at[step])
-    peaks = [gb[i][:, LANES - 1 : LANES] for i in range(NX)]
+    blocks = [gb[i].astype(F32) for i in range(NX)]
+    peaks = [block[:, LANES - 2 : LANES - 1] + block[:, LANES - 1 : LANES] for block in blocks]
     top = jnp.maximum(jnp.maximum(peaks[0], peaks[1]), jnp.maximum(peaks[2], peaks[3]))
     total = jnp.zeros((parts, LANES), F32)
     for i in range(NX):
-        total = total + gb[i] * jnp.exp(peaks[i] - top)
+        total = total + blocks[i] * jnp.exp(peaks[i] - top)
     total = jnp.where(used, total, 0.0) * espb[...].reshape(parts, LANES)
     norm = jnp.sum(total, axis=1, keepdims=True)
     post = total * (1.0 / norm)
     lz[...] = jnp.broadcast_to(top + jnp.log(norm), (parts, LANES))
 
     turned = jnp.concatenate([post, jnp.zeros((LANES - parts, LANES), F32)], axis=0).T
-    high, low = split(turned[: SHIFTS * classes, :parts])
+    both = jnp.concatenate(split(turned[: SHIFTS * classes, :parts]), axis=0)
+    pairs = SHIFTS * classes
     real_side = x < NX // 2
-    at_e = pl.ds(pl.multiple_of(jnp.where(real_side, 0, ck), LANES), ck)
-    at_f = pl.ds(pl.multiple_of(jnp.where(real_side, ck, 0), LANES), ck)
     sign = jnp.where(real_side, -1.0, 1.0).astype(F32) * (1.0 / math.sqrt(npart))
     scale = 1.0 / math.sqrt(npart)
-    for piece in range(NQ // 2):
-        q = (x % 2) * (NQ // 2) + piece
-        e_rows = pb[:, q, :, at_e].reshape(parts, ck)
-        f_rows = pb[:, q, :, at_f].reshape(parts, ck)
-        e = nn(high, e_rows) + nn(low, e_rows)
-        f = nn(high, f_rows) + nn(low, f_rows)
-        for j in range(ck // LANES):
-            at_table = q * (ck // LANES) + j
+    half = ck // 2
+    for piece in range(NQ):
+        place = (x % 2) * NQ + piece
+        q = place // 2
+        within = (place % 2) * half
+        at_e = pl.ds(pl.multiple_of(within + jnp.where(real_side, 0, ck), LANES), half)
+        at_f = pl.ds(pl.multiple_of(within + jnp.where(real_side, ck, 0), LANES), half)
+        e = nn(both, pb[:, q, :, at_e].reshape(parts, half))
+        f = nn(both, pb[:, q, :, at_f].reshape(parts, half))
+        e = e[:pairs] + e[pairs:]
+        f = f[:pairs] + f[pairs:]
+        for j in range(half // LANES):
+            at_table = place * (half // LANES) + j
 
             def of(table, t):
                 return table[t * classes : (t + 1) * classes, j * LANES : (j + 1) * LANES]
@@ -419,27 +439,17 @@
                 sine = tab[at_table, 2 * i + 1 : 2 * i + 2, :]
                 even = even + cosine * (of(e, plus) + of(e, minus))
                 odd = odd + sine * (of(f, plus) - of(f, minus))
-            at_column = piece * ck + j * LANES
+            at_column = piece * half + j * LANES
             cb[:, at_column : at_column + LANES] = scale * even + sign * odd
 
-    width = 2 * coefs // NX
-    cols = width // LANES
-    spread = LANES // classes
-    k = lax.broadcasted_iota(jnp.int32, (spread, width), 1)
-    keep = k % cols == lax.broadcasted_iota(jnp.int32, (spread, width), 0)
-    d = lax.broadcasted_iota(jnp.int32, (LANES, width), 0)
-    first = ((d // 32) * 32 + (d % 16) * 2 + (d // 16) % 2) * cols
-    k = lax.broadcasted_iota(jnp.int32, (LANES, width), 1)
-    pick = jnp.where((k >= first) & (k < first + cols), 1.0, 0.0).astype(BF16)
     laid = jnp.concatenate(
         [
-            jnp.where(keep, jnp.broadcast_to(cb[i : i + 1, :], (spread, width)), 0.0)
+            (jnp.broadcast_to(cb[i : i + 1, :], (spread, width)) * keep[...]).astype(BF16)
             for i in [0, *range(classes - 1, 0, -1)]
         ],
         axis=0,
     )
-    high, low = split(laid)
-    wb[...] = (nt(pick, high) + nt(pick, low)).reshape(NG, NZ, LANES)
+    wb[...] = nt(pick[...], laid).reshape(NG, NZ, LANES).astype(BF16)
     for step in range(1, NG):
         other = (group + step) % NG
         go(
@@ -457,7 +467,7 @@
         src = (group + step) % NG
         arrived(yb.at[src], r_w.at[src])
     heard(3)
-    tb[...] = jnp.sum(yb[...], axis=0).reshape(NZ, 1, LANES)
+    tb[...] = jnp.sum(yb[...].astype(F32), axis=0).reshape(NZ, 1, LANES)
     for step in range(1, NZ):
         other = (z + step) % NZ
         go(remote(tb.at[other], zb.at[z], s_z.at[step], r_z.at[z], me, other * 2 + yh))
@@ -497,7 +507,7 @@
         width = both // NX
         cols = width // LANES
         npart = rows * NX * NS * 2 * NZ
-        assert ck % LANES == 0 and refs * NS == LANES and SHIFTS * classes < LANES
+        assert ck % LANES == 0 and refs * NS == LANES and SHIFTS * classes < LANES - 1 and ck % (2 * LANES) == 0
         dma = pltpu.SemaphoreType.DMA
         log_post, class_sums = pl.pallas_call(
             functools.partial(kernel, coefs, npart, rows, refs, classes, orients),
@@ -526,12 +536,15 @@
                 pltpu.VMEM((LANES, LANES), F32),
                 pltpu.VMEM((rows, LANES), F32),
                 pltpu.VMEM((NX, rows, LANES), F32),
-                pltpu.VMEM((NX, parts, LANES), F32),
+                pltpu.VMEM((NX, parts, LANES), BF16),
                 pltpu.VMEM((parts, LANES), F32),
+                pltpu.VMEM((LANES, SHIFTS * LANES), BF16),
+                pltpu.VMEM((LANES // classes, width), F32),
+                pltpu.VMEM((LANES, width), BF16),
                 pltpu.VMEM((NX, SHIFTS, rows, LANES), F32),
                 pltpu.VMEM((classes, width), F32),
-                pltpu.VMEM((NG, NZ, LANES), F32),
-                pltpu.VMEM((NG, NZ, LANES), F32),
+                pltpu.VMEM((NG, NZ, LANES), BF16),
+                pltpu.VMEM((NG, NZ, LANES), BF16),
                 pltpu.VMEM((NZ, 1, LANES), F32),
                 pltpu.VMEM((NZ, 1, LANES), F32),
                 pltpu.SemaphoreType.REGULAR((4,)),

time: 51.9 us -> 49.6 us (0.956)
  Pallas kernels: 48.8 us -> 46.5 us
    pallas_call x1, Pallas kernels: 48.8 us -> 46.5 us  [local(): pl.pallas_call(functools.partial(kernel, coefs, npart, rows, refs, classe...]
where the time goes in v2:
time: 49.6 us; the launch traced here: 49.4 us
  Pallas kernels  46.5 us (94%)
  local copies, waits for them, and re-layouts  2.29 us (5%)
  between operations  0.65 us (1%)
    pallas_call x1, Pallas kernels, local(): pl.pallas_call(functools.partial(kernel, coefs, npart, rows, refs, classe...  46.5 us
    unnamed x4, local copies, waits for them, and re-layouts  2.29 us

profile of v2, /device:TPU:1, one launch (start us, length us, event | category | flops | bytes accessed | tf_op | source)
XLA Modules:
  0.0 49.4 jit_solution(13843219800430360763)
XLA Ops:
  0.6 46.5 %expectation.1 = (f32[9,16,512]{2,1,0:T(8,128)}, f32[8,14]{1,0:T(8,128)}) custom-call(s32[16]{0:T(128)} %off_hbm.1, f32[8]{0:T(128)} %clp_hbm.1, f32[64]{0:T(128)} %olp_hbm.1, bf16[16,7168]{1,0:T(8,128)(2,1)} %part_hbm.1, bf16[32,7168]{1,0:T(8,128)(2,1)} %refs_hbm.1, f32[28,128]{1,0:T(8,128)} %bitcast.5, s32[4,128]{1,0:T(4,128)} %bitcast.6, ...), custom_call_target="tpu_custom_call" | custom-call | tf_op jit(solution)/shard_map/expectation/pallas_call | solution.py:512
  47.1 0.0 copy-start
  47.1 1.7 %copy.13 = f32[16,9,512]{2,0,1:T(8,128)} copy(f32[16,9,512]{2,0,1:T(8,128)} %bitcast.4) | data formatting | bytes 589824
  48.8 0.0 copy-done
  48.8 0.6 %copy.14 = f32[8,14]{1,0:T(8,128)} copy(f32[8,14]{1,0:T(8,128)S(1)} %copy-done) | data formatting | bytes 896
Async XLA Ops:
  47.1 1.7 %copy-start = (f32[8,14]{1,0:T(8,128)S(1)}, f32[8,14]{1,0:T(8,128)}, u32[]{:S(2)}) copy-start(f32[8,14]{1,0:T(8,128)} %get-tuple-element.9) | copy-start | bytes 1348

commit v3 on v2

--- a/solution.py
+++ b/solution.py
@@ -16,6 +16,8 @@
 NZ = 16
 NG = 8
 NQ = 7
+NEAR_LAG = 2
+FAR_LAG = 4
 AHEAD = 5
 LANES = 128
 F32 = jnp.float32
@@ -79,6 +81,7 @@
     pb,
     rb,
     sp,
+    sp_far,
     s,
     na,
     spv,
@@ -136,6 +139,7 @@
     opposite = (me + 2 * NS) % (NX * NS)
     xl = (x + NX - 1) % NX
     xr = (x + 1) % NX
+    xo = (x + 2) % NX
     partner = me + 1 - 2 * core
     y_ref = me + 2 - 4 * yl
     y_dom = dm + core * (1 - 2 * yh)
@@ -294,17 +298,20 @@
     na[...] = jnp.zeros_like(na)
     s[...] = jnp.zeros_like(s)
 
-    def compute(q):
+    block = SHIFTS * rows
+
+    def turn(to, slot, xs, q):
         def tile(j, carry):
             at_real = pl.ds(pl.multiple_of(j * LANES, LANES), LANES)
             at_imag = pl.ds(pl.multiple_of(ck + j * LANES, LANES), LANES)
             at_table = q * (ck // LANES) + j
-            real = pb[:, q, :, at_real].reshape(NX * rows, LANES).astype(F32)
-            imag = pb[:, q, :, at_imag].reshape(NX * rows, LANES).astype(F32)
+            real = pb[xs, q, :, at_real].astype(F32)
+            imag = pb[xs, q, :, at_imag].astype(F32)
 
             def put(t, turned_real, turned_imag):
-                sp[pl.ds(t * NX * rows, NX * rows), at_real] = turned_real.astype(BF16)
-                sp[pl.ds(t * NX * rows, NX * rows), at_imag] = turned_imag.astype(BF16)
+                at_rows = pl.ds(slot * block + t * rows, rows)
+                to[at_rows, at_real] = turned_real.astype(BF16)
+                to[at_rows, at_imag] = turned_imag.astype(BF16)
 
             plain = tw[at_table, 8:9, :]
             put(4, real * plain, imag * plain)
@@ -315,82 +322,94 @@
                 ic, is_ = imag * cosine, imag * sine
                 put(plus, rc - is_, rs + ic)
                 put(minus, rc + is_, ic - rs)
-            weight = w[pl.ds(at_table, 1), :]
+            return carry
+
+        for j in range(ck // LANES):
+            tile(j, 0)
+
+    def measure(q):
+        def tile(j, carry):
+            at_real = pl.ds(pl.multiple_of(j * LANES, LANES), LANES)
+            at_imag = pl.ds(pl.multiple_of(ck + j * LANES, LANES), LANES)
+            weight = w[pl.ds(q * (ck // LANES) + j, 1), :]
             ref_real = rb[q, :, at_real].astype(F32)
             ref_imag = rb[q, :, at_imag].astype(F32)
             na[...] += weight * (ref_real * ref_real + ref_imag * ref_imag)
             return carry
 
         lax.fori_loop(0, ck // LANES, tile, 0)
-        s[...] += nt(sp[...], rb[q])
+
+    near_rows = 3 * block
+
+    def score_near(q):
+        s[0:near_rows, :] += nt(sp[q], rb[q])
+
+    def score_far(q):
+        arrived(pb.at[xo, q], r_opp.at[q])
+        turn(sp_far, 0, xo, q)
+        s[near_rows:, :] += nt(sp_far[...], rb[q])
 
     def forward_refs(q):
         arrived(rb.at[q, y_rows], r_y.at[q])
         there = rb.at[q, y_rows]
         go(remote(there, there, s_py.at[q], r_py.at[q], partner, dm))
 
-    def ready(q):
+    def other_side(q):
         if q % 2 == 0:
             arrived(pb.at[xr, q], r_right.at[q])
         else:
             arrived(pb.at[xl, q], r_left.at[q])
-        arrived(pb.at[xl, q], r_opp.at[q])
-        arrived(rb.at[q, p_rows], r_p.at[q])
-        arrived(rb.at[q, py_rows], r_py.at[q])
-
-    forward(0)
-    send_own(AHEAD)
-    forward_refs(0)
-    heard(0)
-    tell(1)
-    forward(1)
-    for q in range(AHEAD + 1, NQ):
-        send_own(q)
-    forward_refs(1)
-    forward(2)
-    forward(3)
+
     for q in range(NQ):
-        if q + 2 < NQ:
-            forward_refs(q + 2)
-        ready(q)
-        if q + 4 < NQ:
-            forward(q + 4)
-        compute(q)
+        turn(sp.at[q], 0, x, q)
+    for q in range(NQ + FAR_LAG):
+        if q < NQ:
+            forward(q)
+            if q == 0:
+                send_own(AHEAD)
+            if q == 1:
+                for later in range(AHEAD + 1, NQ):
+                    send_own(later)
+            forward_refs(q)
+            other_side(q)
+            turn(sp.at[q], 1, xl, q)
+            turn(sp.at[q], 2, xr, q)
+        if 0 <= q - NEAR_LAG < NQ:
+            arrived(rb.at[q - NEAR_LAG, p_rows], r_p.at[q - NEAR_LAG])
+            arrived(rb.at[q - NEAR_LAG, py_rows], r_py.at[q - NEAR_LAG])
+            score_near(q - NEAR_LAG)
+            measure(q - NEAR_LAG)
+        if q >= FAR_LAG:
+            score_far(q - FAR_LAG)
         if q == 1:
+            heard(0)
+            tell(1)
+        if q == 4:
             heard(1)
             tell(2)
-        if q == 4:
-            heard(2)
-            tell(3)
+    heard(2)
+    tell(3)
 
     norm_row = jnp.sum(na[...].T, axis=0, keepdims=True)
     s[...] += prior - norm_row
     parts = NX * rows
-    peak = s[0:parts, :]
-    for t in range(1, SHIFTS):
-        peak = jnp.maximum(peak, s[t * parts : (t + 1) * parts, :])
+    s4 = s.reshape(NX, SHIFTS, rows, LANES)
+    by_shift = [s4[:, t].reshape(parts, LANES) for t in range(SHIFTS)]
+    peak = functools.reduce(jnp.maximum, by_shift)
     peak = jnp.max(peak, axis=1, keepdims=True)
     peak_high, peak_low = split(peak)
     peak = peak_high.astype(F32) + peak_low.astype(F32)
-    powers = [jnp.exp(s[t * parts : (t + 1) * parts, :] - peak).astype(BF16) for t in range(SHIFTS)]
+    powers = [jnp.exp(value - peak).astype(BF16) for value in by_shift]
     sums = nt(jnp.concatenate(powers, axis=1), chosen[...])
     tail = jnp.where(lane < LANES - 1, peak_high.astype(F32), peak_low.astype(F32))
-    gb[x] = jnp.where(used, sums, tail).astype(BF16)
+    packed = jnp.where(used, sums, tail).astype(BF16)
+    for slot, xs in enumerate((x, xl, xr, xo)):
+        gb[x, pl.ds(pl.multiple_of(xs * rows, rows), rows), :] = packed[slot * rows : (slot + 1) * rows]
     for step, peer in enumerate((right, left, opposite)):
         go(remote(gb.at[x], gb.at[x], s_g.at[step], r_g.at[step], peer, dm))
-    s4 = s.reshape(SHIFTS, NX, rows, LANES)
-    for step, peer in enumerate((right, left, opposite)):
-        go(
-            remote(
-                s4.at[:, (x + (1, NX - 1, 2)[step]) % NX],
-                sr.at[x],
-                s_s.at[step],
-                r_s.at[step],
-                peer,
-                dm,
-            )
-        )
-    sr[x] = s4[:, x]
+    for step, (slot, peer) in enumerate(((2, right), (1, left), (3, opposite))):
+        go(remote(s4.at[slot], sr.at[x], s_s.at[step], r_s.at[step], peer, dm))
+    sr[x] = s4[0]
 
     for step in range(3):
         src = (x + (NX - 1, 1, 2)[step]) % NX
@@ -509,6 +528,10 @@
         npart = rows * NX * NS * 2 * NZ
         assert ck % LANES == 0 and refs * NS == LANES and SHIFTS * classes < LANES - 1 and ck % (2 * LANES) == 0
         dma = pltpu.SemaphoreType.DMA
+
+        def hbm(array):
+            return pltpu.with_memory_space_constraint(array, pltpu.HBM)
+
         log_post, class_sums = pl.pallas_call(
             functools.partial(kernel, coefs, npart, rows, refs, classes, orients),
             out_shape=(
@@ -531,7 +554,8 @@
                 pltpu.VMEM((coefs // LANES, 16, LANES), F32),
                 pltpu.VMEM((NX, NQ, rows, 2 * ck), BF16),
                 pltpu.VMEM((NQ, LANES, 2 * ck), BF16),
-                pltpu.VMEM((SHIFTS * parts, 2 * ck), BF16),
+                pltpu.VMEM((NQ, SHIFTS * 3 * rows, 2 * ck), BF16),
+                pltpu.VMEM((SHIFTS * rows, 2 * ck), BF16),
                 pltpu.VMEM((SHIFTS * parts, LANES), F32),
                 pltpu.VMEM((LANES, LANES), F32),
                 pltpu.VMEM((rows, LANES), F32),
@@ -555,19 +579,19 @@
             + [dma((NG,))] * 2
             + [dma((NZ,))] * 2,
             compiler_params=pltpu.CompilerParams(
-                collective_id=0, has_side_effects=True, vmem_limit_bytes=67043328
+                collective_id=0, has_side_effects=True, vmem_limit_bytes=32 * 1024 * 1024
             ),
             name="expectation",
         )(
-            offsets,
-            class_logprior,
-            orient_logprior,
-            particles,
-            references,
-            noise_weight.reshape(coefs // LANES, LANES),
-            ref_class.reshape(NX, LANES),
-            ref_orient.reshape(NX, LANES),
-            jnp.asarray(phase_tables(coefs)),
+            hbm(offsets),
+            hbm(class_logprior),
+            hbm(orient_logprior),
+            hbm(particles),
+            hbm(references),
+            hbm(noise_weight.reshape(coefs // LANES, LANES)),
+            hbm(ref_class.reshape(NX, LANES)),
+            hbm(ref_orient.reshape(NX, LANES)),
+            hbm(jnp.asarray(phase_tables(coefs))),
         )
         return jnp.swapaxes(log_post, 0, 1), class_sums
 

time: 49.6 us -> 45.9 us (0.925)
  Pallas kernels: 46.5 us -> 43.8 us
  local copies, waits for them, and re-layouts: 2.29 us -> 1.31 us
    pallas_call x1, Pallas kernels: 46.5 us -> 43.8 us  [local(): pl.pallas_call(functools.partial(kernel, coefs, npart, rows, refs, classe...]
    unnamed x4 -> x2, local copies, waits for them, and re-layouts: 2.29 us -> 1.31 us
where the time goes in v3:
time: 45.9 us; the launch traced here: 45.7 us
  Pallas kernels  43.8 us (95%)
  local copies, waits for them, and re-layouts  1.31 us (3%)
  between operations  0.64 us (1%)
    pallas_call x1, Pallas kernels, local(): pl.pallas_call(functools.partial(kernel, coefs, npart, rows, refs, classe...  43.8 us
    unnamed x2, local copies, waits for them, and re-layouts  1.31 us

profile of v3, /device:TPU:1, one launch (start us, length us, event | category | flops | bytes accessed | tf_op | source)
XLA Modules:
  0.0 45.7 jit_solution(13487167941458958331)
XLA Ops:
  0.6 43.8 %expectation.1 = (f32[9,16,512]{2,1,0:T(8,128)S(1)}, f32[8,14]{1,0:T(8,128)S(1)}) custom-call(s32[16]{0:T(128)} %off_hbm.1, f32[8]{0:T(128)} %clp_hbm.1, f32[64]{0:T(128)} %olp_hbm.1, bf16[16,7168]{1,0:T(8,128)(2,1)} %part_hbm.1, bf16[32,7168]{1,0:T(8,128)(2,1)} %refs_hbm.1, f32[28,128]{1,0:T(8,128)} %bitcast.5, s32[4,128]{1,0:T(4,128)} %bitcast.6, ...), custom_call_target="tpu_custom_call" | custom-call | tf_op jit(solution)/shard_map/expectation/pallas_call | solution.py:535
  44.4 0.7 %copy.13 = f32[16,9,512]{2,0,1:T(8,128)} copy(f32[16,9,512]{2,0,1:T(8,128)S(1)} %bitcast.4) | data formatting | bytes 589824
  45.1 0.6 %copy.14 = f32[8,14]{1,0:T(8,128)} copy(f32[8,14]{1,0:T(8,128)S(1)} %get-tuple-element.9) | data formatting | bytes 896

commit v4 on v3

--- a/solution.py
+++ b/solution.py
@@ -16,9 +16,8 @@
 NZ = 16
 NG = 8
 NQ = 7
-NEAR_LAG = 2
-FAR_LAG = 4
-AHEAD = 5
+NEAR_LAG = 1
+HELD = 2
 LANES = 128
 F32 = jnp.float32
 BF16 = jnp.bfloat16
@@ -232,9 +231,15 @@
     def forward(q):
         if q % 2 == 0:
             arrived(pb.at[xl, q], r_left.at[q])
+        if q % 2 == 1 or q == NQ - 1:
+            arrived(pb.at[xr, q], r_right.at[q])
+        if q == NQ - 1:
+            for way, (xs, peer) in enumerate(((xl, right), (xr, left))):
+                piece = pb.at[xs, q, :, way * ck : (way + 1) * ck]
+                go(remote(piece, piece, s_fwd.at[q + way], r_opp.at[q + way], peer, dm))
+        elif q % 2 == 0:
             go(remote(pb.at[xl, q], pb.at[xl, q], s_fwd.at[q], r_opp.at[q], right, dm))
         else:
-            arrived(pb.at[xr, q], r_right.at[q])
             go(remote(pb.at[xr, q], pb.at[xr, q], s_fwd.at[q], r_opp.at[q], left, dm))
 
     y_rows = pl.ds(pl.multiple_of((y_ref % NS) * refs, refs), refs)
@@ -244,8 +249,7 @@
 
     for q in range(NQ):
         arrived(pb.at[x, q], lp.at[q])
-        if q < AHEAD:
-            send_own(q)
+        send_own(q)
         arrived(rb.at[q, own_rows], lr.at[q])
         own = rb.at[q, own_rows]
         go(remote(own, own, s_y.at[q], r_y.at[q], y_ref, y_dom))
@@ -345,7 +349,11 @@
         s[0:near_rows, :] += nt(sp[q], rb[q])
 
     def score_far(q):
-        arrived(pb.at[xo, q], r_opp.at[q])
+        if q == NQ - 1:
+            for way in range(2):
+                arrived(pb.at[xo, q, :, way * ck : (way + 1) * ck], r_opp.at[q + way])
+        else:
+            arrived(pb.at[xo, q], r_opp.at[q])
         turn(sp_far, 0, xo, q)
         s[near_rows:, :] += nt(sp_far[...], rb[q])
 
@@ -354,69 +362,79 @@
         there = rb.at[q, y_rows]
         go(remote(there, there, s_py.at[q], r_py.at[q], partner, dm))
 
+    def refs_ready(q):
+        arrived(rb.at[q, p_rows], r_p.at[q])
+        arrived(rb.at[q, py_rows], r_py.at[q])
+
     def other_side(q):
-        if q % 2 == 0:
+        if q % 2 == 0 and q < NQ - 1:
             arrived(pb.at[xr, q], r_right.at[q])
-        else:
+        elif q % 2 == 1:
             arrived(pb.at[xl, q], r_left.at[q])
 
     for q in range(NQ):
         turn(sp.at[q], 0, x, q)
-    for q in range(NQ + FAR_LAG):
-        if q < NQ:
-            forward(q)
-            if q == 0:
-                send_own(AHEAD)
-            if q == 1:
-                for later in range(AHEAD + 1, NQ):
-                    send_own(later)
-            forward_refs(q)
-            other_side(q)
-            turn(sp.at[q], 1, xl, q)
-            turn(sp.at[q], 2, xr, q)
-        if 0 <= q - NEAR_LAG < NQ:
-            arrived(rb.at[q - NEAR_LAG, p_rows], r_p.at[q - NEAR_LAG])
-            arrived(rb.at[q - NEAR_LAG, py_rows], r_py.at[q - NEAR_LAG])
+    for q in range(NQ):
+        forward(q)
+        forward_refs(q)
+        other_side(q)
+        turn(sp.at[q], 1, xl, q)
+        turn(sp.at[q], 2, xr, q)
+        if q >= NEAR_LAG:
+            refs_ready(q - NEAR_LAG)
             score_near(q - NEAR_LAG)
             measure(q - NEAR_LAG)
-        if q >= FAR_LAG:
-            score_far(q - FAR_LAG)
         if q == 1:
             heard(0)
             tell(1)
         if q == 4:
             heard(1)
             tell(2)
+    for q in range(NQ - NEAR_LAG, NQ):
+        refs_ready(q)
+        score_near(q)
+        measure(q)
+    for q in range(NQ - HELD):
+        score_far(q)
     heard(2)
     tell(3)
 
-    norm_row = jnp.sum(na[...].T, axis=0, keepdims=True)
-    s[...] += prior - norm_row
+    bias = prior - jnp.sum(na[...].T, axis=0, keepdims=True)
+    s4 = s.reshape(NX, SHIFTS, rows, LANES)
+
+    def settle(first, last):
+        count = (last - first) * rows
+        s4[first:last] += bias
+        by_shift = [s4[first:last, t].reshape(count, LANES) for t in range(SHIFTS)]
+        peak = functools.reduce(jnp.maximum, by_shift)
+        peak = jnp.max(peak, axis=1, keepdims=True)
+        peak_high, peak_low = split(peak)
+        peak = peak_high.astype(F32) + peak_low.astype(F32)
+        powers = [jnp.exp(value - peak).astype(BF16) for value in by_shift]
+        sums = nt(jnp.concatenate(powers, axis=1), chosen[...])
+        tail = jnp.where(lane < LANES - 1, peak_high.astype(F32), peak_low.astype(F32))
+        packed = jnp.where(used, sums, tail).astype(BF16)
+        for slot in range(first, last):
+            xs = (x, xl, xr, xo)[slot]
+            place = pl.ds(pl.multiple_of(xs * rows, rows), rows)
+            gb[x, place, :] = packed[(slot - first) * rows : (slot - first + 1) * rows]
+
+    settle(0, NX - 1)
+    for q in range(NQ - HELD, NQ):
+        score_far(q)
+    settle(NX - 1, NX)
     parts = NX * rows
-    s4 = s.reshape(NX, SHIFTS, rows, LANES)
-    by_shift = [s4[:, t].reshape(parts, LANES) for t in range(SHIFTS)]
-    peak = functools.reduce(jnp.maximum, by_shift)
-    peak = jnp.max(peak, axis=1, keepdims=True)
-    peak_high, peak_low = split(peak)
-    peak = peak_high.astype(F32) + peak_low.astype(F32)
-    powers = [jnp.exp(value - peak).astype(BF16) for value in by_shift]
-    sums = nt(jnp.concatenate(powers, axis=1), chosen[...])
-    tail = jnp.where(lane < LANES - 1, peak_high.astype(F32), peak_low.astype(F32))
-    packed = jnp.where(used, sums, tail).astype(BF16)
-    for slot, xs in enumerate((x, xl, xr, xo)):
-        gb[x, pl.ds(pl.multiple_of(xs * rows, rows), rows), :] = packed[slot * rows : (slot + 1) * rows]
     for step, peer in enumerate((right, left, opposite)):
         go(remote(gb.at[x], gb.at[x], s_g.at[step], r_g.at[step], peer, dm))
-    for step, (slot, peer) in enumerate(((2, right), (1, left), (3, opposite))):
-        go(remote(s4.at[slot], sr.at[x], s_s.at[step], r_s.at[step], peer, dm))
-    sr[x] = s4[0]
-
     for step in range(3):
         src = (x + (NX - 1, 1, 2)[step]) % NX
         arrived(espb.at[src], r_e.at[step])
     for step in range(3):
         src = (x + (NX - 1, 1, 2)[step]) % NX
         arrived(gb.at[src], r_g.at[step])
+    for step, (slot, peer) in enumerate(((2, right), (1, left), (3, opposite))):
+        go(remote(s4.at[slot], sr.at[x], s_s.at[step], r_s.at[step], peer, dm))
+    sr[x] = s4[0]
     blocks = [gb[i].astype(F32) for i in range(NX)]
     peaks = [block[:, LANES - 2 : LANES - 1] + block[:, LANES - 1 : LANES] for block in blocks]
     top = jnp.maximum(jnp.maximum(peaks[0], peaks[1]), jnp.maximum(peaks[2], peaks[3]))
@@ -501,6 +519,8 @@
         for i in range(NX):
             post_out[t, :, i * LANES : (i + 1) * LANES] = sr[i, t] + bias
 
+    for copy in sends:
+        copy.wait_send()
     for step in range(1, NZ):
         src = (z + step) % NZ
         arrived(zb.at[src], r_z.at[src])
@@ -508,8 +528,17 @@
     final = jnp.broadcast_to(final, (classes, LANES))
     final = pltpu.roll(final, 0, 1, stride=spread, stride_axis=0)
     sums_out[...] = final[:, :cols]
-    for copy in sends:
-        copy.wait_send()
+
+
+def store(post, sums, post_out, sums_out, sems):
+    copies = [
+        pltpu.make_async_copy(post, post_out, sems.at[0]),
+        pltpu.make_async_copy(sums, sums_out, sems.at[1]),
+    ]
+    for copy in copies:
+        copy.start()
+    for copy in copies:
+        copy.wait()
 
 
 def solution(mesh):
@@ -574,7 +603,7 @@
                 pltpu.SemaphoreType.REGULAR((4,)),
                 dma((7,)),
             ]
-            + [dma((NQ,))] * 14
+            + [dma((NQ + 1,))] * 14
             + [dma((3,))] * 6
             + [dma((NG,))] * 2
             + [dma((NZ,))] * 2,
@@ -593,6 +622,18 @@
             hbm(ref_orient.reshape(NX, LANES)),
             hbm(jnp.asarray(phase_tables(coefs))),
         )
+        log_post, class_sums = pl.pallas_call(
+            store,
+            out_shape=(
+                jax.ShapeDtypeStruct(log_post.shape, F32),
+                jax.ShapeDtypeStruct(class_sums.shape, F32),
+            ),
+            in_specs=[pl.BlockSpec(memory_space=pltpu.VMEM)] * 2,
+            out_specs=[pl.BlockSpec(memory_space=pltpu.HBM)] * 2,
+            scratch_shapes=[dma((2,))],
+            compiler_params=pltpu.CompilerParams(vmem_limit_bytes=1024 * 1024),
+            name="store",
+        )(log_post, class_sums)
         return jnp.swapaxes(log_post, 0, 1), class_sums
 
     return jax.shard_map(

time: 45.9 us -> 44.7 us (0.974)
  local copies, waits for them, and re-layouts: 1.31 us -> 0 us
    unnamed x2 -> x0, local copies, waits for them, and re-layouts: 1.31 us -> none
    pallas_call x0 -> x1, Pallas kernels: none -> 0.74 us  [local(): pl.pallas_call(store, out_shape=(jax.ShapeDtypeStruct(log_post.shape, F32...]
    pallas_call x1, Pallas kernels: 43.8 us -> 43.2 us  [local(): pl.pallas_call(functools.partial(kernel, coefs, npart, rows, refs, classe...]
where the time goes in v4:
time: 44.7 us; the launch traced here: 44.6 us
  Pallas kernels  43.9 us (98%)
  between operations  0.64 us (1%)
    pallas_call x1, Pallas kernels, local(): pl.pallas_call(functools.partial(kernel, coefs, npart, rows, refs, classe...  43.2 us

profile of v4, /device:TPU:1, one launch (start us, length us, event | category | flops | bytes accessed | tf_op | source)
XLA Modules:
  0.0 44.6 jit_solution(10501051210129662350)
XLA Ops:
  0.6 43.2 %expectation.1 = (f32[9,16,512]{2,1,0:T(8,128)S(1)}, f32[8,14]{1,0:T(8,128)S(1)}) custom-call(s32[16]{0:T(128)} %off_hbm.1, f32[8]{0:T(128)} %clp_hbm.1, f32[64]{0:T(128)} %olp_hbm.1, bf16[16,7168]{1,0:T(8,128)(2,1)} %part_hbm.1, bf16[32,7168]{1,0:T(8,128)(2,1)} %refs_hbm.1, f32[28,128]{1,0:T(8,128)} %bitcast.4, s32[4,128]{1,0:T(4,128)} %bitcast.5, ...), custom_call_target="tpu_custom_call" | custom-call | tf_op jit(solution)/shard_map/expectation/pallas_call | solution.py:564
  43.8 0.7 %store.1 = (f32[9,16,512]{2,1,0:T(8,128)}, f32[8,14]{1,0:T(8,128)}) custom-call(f32[9,16,512]{2,1,0:T(8,128)S(1)} %get-tuple-element.6.post, f32[8,14]{1,0:T(8,128)S(1)} %get-tuple-element.7.sums), custom_call_target="tpu_custom_call" | custom-call | tf_op jit(solution)/shard_map/store/pallas_call | solution.py:625

commit v5 on v4

--- a/solution.py
+++ b/solution.py
@@ -97,6 +97,7 @@
     tb,
     zb,
     far,
+    plane,
     sm,
     lp,
     lr,
@@ -157,6 +158,33 @@
     def arrived(buffer, sem):
         pltpu.make_async_copy(buffer, buffer, sem).wait()
 
+    barrier = pltpu.get_barrier_semaphore()
+
+    def beside(distance, act):
+        @pl.when(z >= distance)
+        def _():
+            act(me, dm - 2 * distance)
+
+        @pl.when(z + distance < NZ)
+        def _():
+            act(me, dm + 2 * distance)
+
+    def near(distance):
+        return (z + NZ - distance) // NZ + (2 * NZ - 1 - z - distance) // NZ
+
+    def greet(ref, dom):
+        pl.semaphore_signal(barrier, inc=1, device_id=(ref, dom), device_id_type=MESH)
+
+    y = yh * 2 + yl
+    neighbours = [(right, dm), (left, dm), (partner, dm)]
+    for turned in (1, 3):
+        other_y = (y + turned) % 4
+        for swap in range(2):
+            other_core = (core + swap) % 2
+            neighbours.append((x * NS + (other_y % 2) * 2 + other_core, z * 2 + other_y // 2))
+    for ref, dom in neighbours:
+        greet(ref, dom)
+    beside(1, greet)
     smalls = (
         (off_hbm, off),
         (clp_hbm, clp),
@@ -181,31 +209,10 @@
             ).start()
     for i, (src, dst) in enumerate(smalls):
         pltpu.make_async_copy(src, dst, sm.at[i]).start()
-
-    barrier = pltpu.get_barrier_semaphore()
-
-    def beside(distance, act):
-        @pl.when(z >= distance)
-        def _():
-            act(me, dm - 2 * distance)
-
-        @pl.when(z + distance < NZ)
-        def _():
-            act(me, dm + 2 * distance)
-
-    def near(distance):
-        return (z + NZ - distance) // NZ + (2 * NZ - 1 - z - distance) // NZ
-
-    def greet(ref, dom):
-        pl.semaphore_signal(barrier, inc=1, device_id=(ref, dom), device_id_type=MESH)
-
-    for step in range(1, NX):
-        greet((me + step * NS) % (NX * NS), dm)
-    for step in range(1, NG):
-        other = (group + step) % NG
-        greet(x * NS + other // 2, z * 2 + other % 2)
-    beside(1, greet)
-    pl.semaphore_wait(barrier, NX - 1 + NG - 1 + near(1))
+    pl.semaphore_wait(barrier, len(neighbours) + near(1))
+
+    for ref, dom in neighbours:
+        pl.semaphore_signal(plane, inc=1, device_id=(ref, dom), device_id_type=MESH)
 
     def tell(i):
         def one(ref, dom):
@@ -229,7 +236,7 @@
         go(remote(pb.at[x, q], pb.at[x, q], s_left.at[q], r_right.at[q], left, dm))
 
     def forward(q):
-        if q % 2 == 0:
+        if q % 2 == 0 or q == NQ - 1:
             arrived(pb.at[xl, q], r_left.at[q])
         if q % 2 == 1 or q == NQ - 1:
             arrived(pb.at[xr, q], r_right.at[q])
@@ -275,8 +282,6 @@
         spv[n : n + 1, :] = -0.5 * (apart_right * apart_right + apart_down * apart_down)
     used = lane < SHIFTS * classes
     espb[x] = jnp.where(used, jnp.exp(spv[...]), 0.0)
-    for step, peer in enumerate((right, left, opposite)):
-        go(remote(espb.at[x], espb.at[x], s_e.at[step], r_e.at[step], peer, dm))
     class_row = cls[pl.ds(x, 1), :]
     orient_row = ori[pl.ds(x, 1), :]
     prior = jnp.zeros((1, LANES), F32)
@@ -369,7 +374,7 @@
     def other_side(q):
         if q % 2 == 0 and q < NQ - 1:
             arrived(pb.at[xr, q], r_right.at[q])
-        elif q % 2 == 1:
+        elif q % 2 == 1 and q < NQ - 1:
             arrived(pb.at[xl, q], r_left.at[q])
 
     for q in range(NQ):
@@ -385,6 +390,9 @@
             score_near(q - NEAR_LAG)
             measure(q - NEAR_LAG)
         if q == 1:
+            pl.semaphore_wait(plane, len(neighbours))
+            for step, peer in enumerate((right, left, opposite)):
+                go(remote(espb.at[x], espb.at[x], s_e.at[step], r_e.at[step], peer, dm))
             heard(0)
             tell(1)
         if q == 4:
@@ -601,6 +609,7 @@
                 pltpu.VMEM((NZ, 1, LANES), F32),
                 pltpu.VMEM((NZ, 1, LANES), F32),
                 pltpu.SemaphoreType.REGULAR((4,)),
+                pltpu.SemaphoreType.REGULAR,
                 dma((7,)),
             ]
             + [dma((NQ + 1,))] * 14

time: 44.7 us -> 44.4 us (level)
  no operation moved by 1% of the time
where the time goes in v5:
time: 44.4 us; the launch traced here: 44.3 us
  Pallas kernels  43.6 us (98%)
  between operations  0.64 us (1%)
    pallas_call x1, Pallas kernels, local(): pl.pallas_call(functools.partial(kernel, coefs, npart, rows, refs, classe...  42.9 us

profile of v5, /device:TPU:1, one launch (start us, length us, event | category | flops | bytes accessed | tf_op | source)
XLA Modules:
  0.0 44.3 jit_solution(4023539625111262200)
XLA Ops:
  0.6 42.9 %expectation.1 = (f32[9,16,512]{2,1,0:T(8,128)S(1)}, f32[8,14]{1,0:T(8,128)S(1)}) custom-call(s32[16]{0:T(128)} %off_hbm.1, f32[8]{0:T(128)} %clp_hbm.1, f32[64]{0:T(128)} %olp_hbm.1, bf16[16,7168]{1,0:T(8,128)(2,1)} %part_hbm.1, bf16[32,7168]{1,0:T(8,128)(2,1)} %refs_hbm.1, f32[28,128]{1,0:T(8,128)} %bitcast.4, s32[4,128]{1,0:T(4,128)} %bitcast.5, ...), custom_call_target="tpu_custom_call" | custom-call | tf_op jit(solution)/shard_map/expectation/pallas_call | solution.py:572
  43.5 0.7 %store.1 = (f32[9,16,512]{2,1,0:T(8,128)}, f32[8,14]{1,0:T(8,128)}) custom-call(f32[9,16,512]{2,1,0:T(8,128)S(1)} %get-tuple-element.6.post, f32[8,14]{1,0:T(8,128)S(1)} %get-tuple-element.7.sums), custom_call_target="tpu_custom_call" | custom-call | tf_op jit(solution)/shard_map/store/pallas_call | solution.py:634
